TPU v7x, 256 devices: a whole 4x4x8 slice. The times are simulated.
256 devices in a mesh: blk: 128 (over x, z, y), row: 2 (over core).
Axes of the slice: x: 4, y: 4, z: 8, core: 2. Of those that a mesh axis runs over, the one named last changes fastest.
Arguments:
- genotypes: bfloat16 [1024, 128, 2048], P('blk', None, 'row'), may hold values from 0 to 2
- assignment: int32 [128], replicated, may hold values from 0 to 127, each once
- snp_counts: int32 [128], replicated, may hold values from 1024 to 2048, as said below
- basis: float32 [128, 64, 2048], P('blk', None, 'row'), may hold values from -6 to 6
Outputs:
- image: float32 [128, 64, 2048], P('blk', None, 'row')
- new_basis: float32 [128, 64, 2048], P('blk', None, 'row')
- factor: float32 [128, 64, 64], P('blk')
Inputs may be any that keep to these rules, and one draw needn't show every extreme that they name: `assignment`: each block number appears exactly once. `snp_counts`: A block's SNPs fill its leading slots.
All inputs are finite; a program needn't handle non-finite values.
Results may differ from a plain program's by a relative error of at most 0.0021.
Values may be sent and summed in bfloat16 or wider, within the bound.
A program may use at most 64 MiB of HBM per device.

v0:
```python
import jax
import jax.numpy as jnp
from jax import lax
from jax.sharding import PartitionSpec as P

epsilon = 1e-05
shrink_weight = 0.5


def total_of_pieces(array, axis):
    pieces = lax.all_gather(array, axis)
    return pieces.sum(axis=0)


def body(genotypes, assignment, snp_counts, basis):
    ordered = jnp.take(genotypes, assignment, axis=1)
    regrouped = lax.all_to_all(ordered, "blk", split_axis=1, concat_axis=0, tiled=True)
    samples = regrouped.shape[0]
    owned = regrouped.shape[1]
    half_width = regrouped.shape[2]
    block_ids = lax.dynamic_slice_in_dim(assignment, lax.axis_index("blk") * owned, owned)
    catalog = jnp.arange(snp_counts.shape[0], dtype=jnp.int32)
    live_count = jnp.sum(
        jnp.where(block_ids[:, None] == catalog[None, :], snp_counts[None, :], 0), axis=1
    )
    columns = lax.axis_index("row") * half_width + jnp.arange(half_width, dtype=jnp.int32)
    live_mask = columns[None, :] < live_count[:, None]
    values = regrouped.astype(jnp.float32)
    col_mean = jnp.mean(values, axis=0)
    centered = values - col_mean[None]
    col_var = jnp.mean(centered * centered, axis=0)
    standard = jnp.where(
        live_mask[None], centered * lax.rsqrt(col_var + epsilon)[None], 0.0
    ).astype(jnp.bfloat16)
    inverse = 1.0 / samples
    partial_proj = jnp.einsum(
        "nbi,bri->brn",
        standard,
        basis,
        precision=lax.Precision.HIGHEST,
        preferred_element_type=jnp.float32,
    )
    projected = total_of_pieces(partial_proj, "row")
    product = (
        jnp.einsum(
            "nbi,brn->bri",
            standard,
            projected,
            precision=lax.Precision.HIGHEST,
            preferred_element_type=jnp.float32,
        )
        * inverse
    )
    image = shrink_weight * product + (1.0 - shrink_weight) * jnp.where(
        live_mask[:, None, :], basis, 0.0
    )
    gram_part = jnp.einsum("bri,bsi->brs", image, image, precision=lax.Precision.HIGHEST)
    gram_sum = total_of_pieces(gram_part, "row")
    factor = jnp.linalg.cholesky(gram_sum)
    new_basis = jax.scipy.linalg.solve_triangular(factor, image, lower=True)
    return (image, new_basis, factor)


def solution(mesh):
    in_specs = (P("blk", None, "row"), P(), P(), P("blk", None, "row"))
    out_specs = (P("blk", None, "row"), P("blk", None, "row"), P("blk", None, None))
    return jax.shard_map(body, mesh=mesh, in_specs=in_specs, out_specs=out_specs, check_vma=False)
```

profile of v0, /device:TPU:1, one launch (start us, length us, event | category | flops | bytes accessed | tf_op | source)
XLA Modules:
  0.0 113.4 jit_solution(6416810635120617516)
XLA Ops:
  0.6 0.8 compare_select_fusion
  1.5 0.7 compare_and_fusion
  2.1 0.1 copy-done
  2.2 8.1 %gather_fusion = bf16[128,8,1024]{2,0,1:T(8,128)(2,1)} fusion(bf16[8,128,1024]{2,1,0:T(8,128)(2,1)S(1)} %copy-done, s32[1024]{0:T(1024)S(1)} %pad_clamp_fusion), kind=kCustom, calls=%fused_computation | custom fusion | bytes 4194816 | tf_op jit(solution)/shard_map/jit(_take)/gather | solution.py:16
  10.3 1.8 %select_bitcast_fusion = bf16[8,128,1024]{2,1,0:T(8,128)(2,1)S(1)} fusion(bf16[128,8,1024]{2,0,1:T(8,128)(2,1)} %gather_fusion, pred[128]{0:T(512)(128)(4,1)S(1)} %compare_and_fusion), kind=kLoop, calls=%fused_computation.18 | loop fusion | flops 1048576 | bytes 4194432 | tf_op jit(solution)/shard_map/jit(_take)/select_n | solution.py:16
  12.1 2.4 %copy.12 = bf16[8,128,1024]{2,0,1:T(8,128)(2,1)} copy(bf16[8,128,1024]{2,1,0:T(8,128)(2,1)S(1)} %select_bitcast_fusion) | data formatting | bytes 4194304 | tf_op jit(solution)/shard_map/jit(_take)/select_n | solution.py:16
  14.6 17.2 %all-to-all-start = ((bf16[8,128,1024]{2,0,1:T(8,128)(2,1)}), bf16[8,128,1024]{2,0,1:T(8,128)(2,1)}, u32[]{:S(2)}, u32[]{:S(2)}) async-start(bf16[8,128,1024]{2,0,1:T(8,128)(2,1)} %copy.12), calls=%async_computation | async-start | bytes 4194304 | tf_op jit(solution)/shard_map/all_to_all | solution.py:17
  31.8 0.6 dynamic_slice.3
  32.4 1.3 %fusion.40 = s32[]{:T(128)} fusion(s32[128]{0:T(128)S(1)} %copy-done.4, s32[]{:T(128)} %bitcast), kind=kLoop, calls=%fused_computation.50 | loop fusion | flops 383 | bytes 520 | tf_op jit(solution)/shard_map/reduce_sum | solution.py:23
  33.7 0.7 add_compare_fusion
  34.3 46.3 %all-to-all-done = bf16[8,128,1024]{2,0,1:T(8,128)(2,1)} async-done(((bf16[8,128,1024]{2,0,1:T(8,128)(2,1)}), bf16[8,128,1024]{2,0,1:T(8,128)(2,1)}, u32[]{:S(2)}, u32[]{:S(2)}) %all-to-all-start) | async-done | bytes 2097184 | tf_op jit(solution)/shard_map/all_to_all | solution.py:17
  80.6 2.0 %convert_reduce_fusion = f32[1024]{0:T(1024)S(1)} fusion(bf16[8,128,1024]{2,0,1:T(8,128)(2,1)} %all-to-all-done), kind=kLoop, calls=%fused_computation.3 | loop fusion | flops 2096128 | bytes 2101248 | tf_op jit(solution)/shard_map/reduce_sum | solution.py:29
  82.6 2.2 %fusion.10 = f32[1024]{0:T(1024)S(1)} fusion(bf16[8,128,1024]{2,0,1:T(8,128)(2,1)} %all-to-all-done, f32[1024]{0:T(1024)S(1)} %broadcast_multiply_fusion), kind=kLoop, calls=%fused_computation.15 | loop fusion | flops 4193280 | bytes 2105344 | tf_op jit(solution)/shard_map/reduce_sum | solution.py:31
  84.8 3.6 %fusion.21 = f32[64,1024]{1,0:T(8,128)S(1)} fusion(bf16[8,128,1024]{2,0,1:T(8,128)(2,1)} %all-to-all-done, f32[1024]{0:T(1024)S(1)} %add_rsqrt_fusion, f32[1024]{0:T(1024)S(1)} %broadcast_multiply_fusion, pred[1024]{0:T(1024)(128)(4,1)S(1)} %add_compare_fusion, f32[1,64,1024]{2,1,0:T(8,128)S(1)} %copy-done.2), kind=kOutput, calls=%fused_computation.26 | convolution fusion | flops 810549248 | bytes 2630656 | tf_op jit(solution)/shard_map/nbi,bri->brn/dot_general | solution.py:36
  88.4 5.7 %all-gather = f32[128,1024]{1,0:T(8,128)S(1)} all-gather(f32[64,1024]{1,0:T(8,128)S(1)} %fusion.21), channel_id=2, replica_groups=mesh['blk'=128,'row'=2] {'row'}, dimensions={0}, use_global_device_ids=true | all-gather | bytes 786432 | tf_op jit(solution)/shard_map/all_gather | solution.py:11
  94.1 3.0 %fusion.30 = f32[1,64,1024]{2,1,0:T(8,128)S(1)} fusion(f32[64,1024]{1,0:T(8,128)S(1)} %reduce.18, bf16[8,128,1024]{2,0,1:T(8,128)(2,1)} %all-to-all-done, f32[1024]{0:T(1024)S(1)} %add_rsqrt_fusion, f32[1024]{0:T(1024)S(1)} %broadcast_multiply_fusion, pred[1024]{0:T(1024)(128)(4,1)S(1)} %add_compare_fusion, f32[1,64,1024]{2,1,0:T(8,128)S(1)} %copy-done.2), kind=kOutput, calls=%fused_computation.29 | convolution fusion | flops 810811392 | bytes 2892800 | tf_op jit(solution)/shard_map/nbi,brn->bri/dot_general | solution.py:45
  97.1 0.4 fusion.34
  97.5 1.9 %all-gather.1 = f32[128,64]{1,0:T(8,128)S(1)} all-gather(f32[64,64]{1,0:T(8,128)S(1)} %fusion.34), channel_id=3, replica_groups=mesh['blk'=128,'row'=2] {'row'}, dimensions={0}, use_global_device_ids=true | all-gather | bytes 49152 | tf_op jit(solution)/shard_map/all_gather | solution.py:11
  99.5 0.1 copy.14
  99.6 5.8 %custom-call.8 = f32[1,64,64]{2,1,0:T(8,128)S(1)} custom-call(f32[1,64,64]{2,1,0:T(8,128)S(1)} %fusion.37), custom_call_target="Cholesky" | custom-call | tf_op jit(solution)/shard_map/jit(cholesky)/cholesky | solution.py:59
  105.4 0.6 compare_reduce_fusion
  106.1 1.3 %fusion.39 = (f32[1,64,64]{2,1,0:T(8,128)S(1)}, f32[1,64,64]{2,1,0:T(8,128)}) fusion(f32[1,64,64]{2,1,0:T(8,128)S(1)} %custom-call.8, pred[]{:T(512)} %compare_reduce_fusion), kind=kLoop, calls=%fused_computation.41 | loop fusion | flops 16384 | bytes 49153 | tf_op jit(solution)/shard_map/jit(_solve_triangular)/triangular_solve | solution.py:60
  107.4 4.9 %custom-call.9 = f32[1,64,64]{1,2,0:T(8,128)S(1)} custom-call(f32[1,64,64]{2,1,0:T(8,128)S(1)} %get-tuple-element.3), custom_call_target="InvertDiagBlocksLowerTriangular" | custom-call | tf_op jit(solution)/shard_map/jit(_solve_triangular)/triangular_solve | solution.py:60
  112.3 1.1 %convolution_bitcast_fusion = f32[1,64,1024]{2,1,0:T(8,128)} fusion(f32[1,64,1024]{2,1,0:T(8,128)S(1)} %fusion.30, f32[1,64,64]{1,2,0:T(8,128)S(1)} %custom-call.9), kind=kOutput, calls=%fused_computation.25 | convolution fusion | flops 50331648 | bytes 540672 | tf_op jit(solution)/shard_map/jit(_solve_triangular)/triangular_solve | solution.py:60
  (17 shorter events, 0.2 us)
Async XLA Ops:
  0.6 1.6 %copy-start = (bf16[8,128,1024]{2,1,0:T(8,128)(2,1)S(1)}, bf16[8,128,1024]{2,1,0:T(8,128)(2,1)}, u32[]{:S(2)}) copy-start(bf16[8,128,1024]{2,1,0:T(8,128)(2,1)} %param.4) | copy-start | bytes 6291460
  14.6 17.2 %copy-start.3 = (s32[128]{0:T(128)S(1)}, s32[128]{0:T(128)}, u32[]{:S(2)}) copy-start(s32[128]{0:T(128)} %param.5) | copy-start | bytes 1540
  14.6 17.8 %copy-start.4 = (s32[128]{0:T(128)S(1)}, s32[128]{0:T(128)}, u32[]{:S(2)}) copy-start(s32[128]{0:T(128)} %param.6) | copy-start | bytes 1540
  14.6 66.0 %all-to-all-start = ((bf16[8,128,1024]{2,0,1:T(8,128)(2,1)}), bf16[8,128,1024]{2,0,1:T(8,128)(2,1)}, u32[]{:S(2)}, u32[]{:S(2)}) async-start(bf16[8,128,1024]{2,0,1:T(8,128)(2,1)} %copy.12), calls=%async_computation | async-start | bytes 4194304 | tf_op jit(solution)/shard_map/all_to_all | solution.py:17
  34.3 50.5 %copy-start.2 = (f32[1,64,1024]{2,1,0:T(8,128)S(1)}, f32[1,64,1024]{2,1,0:T(8,128)}, u32[]{:S(2)}) copy-start(f32[1,64,1024]{2,1,0:T(8,128)} %param.7) | copy-start | bytes 786436
  97.1 16.3 %copy-start.1 = (f32[1,64,1024]{2,1,0:T(8,128)}, f32[1,64,1024]{2,1,0:T(8,128)S(1)}, u32[]{:S(2)}) copy-start(f32[1,64,1024]{2,1,0:T(8,128)S(1)} %fusion.30) | copy-start | bytes 786436
where the time goes:
time: 114 us; the launch traced here: 113 us
  waiting for transfers between devices  46.3 us (41%)
  other arithmetic  22.1 us (19%)
  starting transfers between devices  17.2 us (15%)
  local copies, waits for them, and re-layouts  11.4 us (10%)
  matrix products  8.12 us (7%)
  blocking collectives  7.54 us (7%)
    all_to_all x1, waiting for transfers between devices, body(): lax.all_to_all(ordered, 'blk', split_axis=1, concat_axis=0, tiled=True)  46.3 us
    all_to_all x1, starting transfers between devices, body(): lax.all_to_all(ordered, 'blk', split_axis=1, concat_axis=0, tiled=True)  17.2 us
    gather x1, local copies, waits for them, and re-layouts, body(): ordered = jnp.take(genotypes, assignment, axis=1)  8.06 us
    all_gather x2, blocking collectives, total_of_pieces(): pieces = lax.all_gather(array, axis)  7.54 us
    another operation x3, other arithmetic, body(): factor = jnp.linalg.cholesky(gram_sum)  6.52 us
    another operation x2, other arithmetic, body(): new_basis = jax.scipy.linalg.solve_triangular(factor, image, lower=True)  6.16 us
    dot_general x1, matrix products, body(): jnp.einsum('nbi,bri->brn', standard, basis, precision=lax.Precision.HIGHE...  3.61 us
    dot_general x1, matrix products, body(): jnp.einsum('nbi,brn->bri', standard, projected, precision=lax.Precision.H...  3.02 us
  transfers between devices with their start and end apart: 1, of which 1 were waited for; matrix products, arithmetic and copies ran while one was open for 2% of the time, Pallas kernels for 0%

commit v1 on v0

--- a/solution.py
+++ b/solution.py
@@ -7,6 +7,12 @@
 shrink_weight = 0.5
 
 
+def swap_blocks(array, axis, split, join):
+    pieces = jnp.split(array, lax.axis_size(axis), axis=split)
+    received = lax.all_to_all(jnp.stack(pieces), axis, 0, 0)
+    return jnp.concatenate(received, axis=join)
+
+
 def total_of_pieces(array, axis):
     pieces = lax.all_gather(array, axis)
     return pieces.sum(axis=0)
@@ -14,7 +20,7 @@
 
 def body(genotypes, assignment, snp_counts, basis):
     ordered = jnp.take(genotypes, assignment, axis=1)
-    regrouped = lax.all_to_all(ordered, "blk", split_axis=1, concat_axis=0, tiled=True)
+    regrouped = swap_blocks(ordered, "blk", 1, 0)
     samples = regrouped.shape[0]
     owned = regrouped.shape[1]
     half_width = regrouped.shape[2]

time: 114 us -> 194 us (1.70)
  local copies, waits for them, and re-layouts: 11.4 us -> 91 us
    unnamed x10 -> x137, local copies, waits for them, and re-layouts: 0.15 us -> 77.1 us
    split x0 -> x7, local copies, waits for them, and re-layouts: none -> 4.45 us  [swap_blocks(): pieces = jnp.split(array, lax.axis_size(axis), axis=split)]
    select_n x1 -> x0, local copies, waits for them, and re-layouts: 2.45 us -> none  [body(): ordered = jnp.take(genotypes, assignment, axis=1)]
  transfers between devices with their start and end apart: 1 -> 1, of which waited for: 1 -> 1; matrix products, arithmetic and copies ran while one was open for 2% -> 1% of each run, Pallas kernels for 0% -> 0%
where the time goes in v1:
time: 194 us; the launch traced here: 193 us
  local copies, waits for them, and re-layouts  91 us (47%)
  waiting for transfers between devices  46.5 us (24%)
  other arithmetic  22.1 us (11%)
  starting transfers between devices  17 us (9%)
  matrix products  8.13 us (4%)
  blocking collectives  7.53 us (4%)
    unnamed x137, local copies, waits for them, and re-layouts  77.1 us
    all_to_all x1, waiting for transfers between devices, swap_blocks(): received = lax.all_to_all(jnp.stack(pieces), axis, 0, 0)  46.5 us
    all_to_all x1, starting transfers between devices, swap_blocks(): received = lax.all_to_all(jnp.stack(pieces), axis, 0, 0)  17 us
    gather x1, local copies, waits for them, and re-layouts, body(): ordered = jnp.take(genotypes, assignment, axis=1)  8.06 us
    all_gather x2, blocking collectives, total_of_pieces(): pieces = lax.all_gather(array, axis)  7.53 us
    another operation x3, other arithmetic, body(): factor = jnp.linalg.cholesky(gram_sum)  6.52 us
    another operation x2, other arithmetic, body(): new_basis = jax.scipy.linalg.solve_triangular(factor, image, lower=True)  6.16 us
    split x7, local copies, waits for them, and re-layouts, swap_blocks(): pieces = jnp.split(array, lax.axis_size(axis), axis=split)  4.45 us
  transfers between devices with their start and end apart: 1, of which 1 were waited for; matrix products, arithmetic and copies ran while one was open for 1% of the time, Pallas kernels for 0%

profile of v1, /device:TPU:1, one launch (start us, length us, event | category | flops | bytes accessed | tf_op | source)
XLA Modules:
  0.0 193.1 jit_solution(16697413153739317817)
XLA Ops:
  0.6 0.8 compare_select_fusion
  1.5 0.7 compare_and_fusion
  2.2 8.1 %gather_fusion = bf16[128,8,1024]{2,0,1:T(8,128)(2,1)} fusion(bf16[8,128,1024]{2,1,0:T(8,128)(2,1)S(1)} %copy-done, s32[1024]{0:T(1024)S(1)} %pad_clamp_fusion), kind=kCustom, calls=%fused_computation | custom fusion | bytes 4194816 | tf_op jit(solution)/shard_map/jit(_take)/gather | solution.py:22
  10.3 1.8 select_bitcast_fusion
  12.6 0.7 fusion.48
  13.3 0.7 fusion.47
  14.0 0.7 fusion.46
  14.7 0.7 fusion.45
  16.0 0.7 fusion.43
  94.3 17.0 %all-to-all-start = ((bf16[128,8,1,1024]{3,1,2,0:T(8,128)(2,1)}), bf16[128,8,1,1024]{3,1,2,0:T(8,128)(2,1)}, u32[]{:S(2)}, u32[]{:S(2)}) async-start(bf16[128,8,1,1024]{3,1,2,0:T(8,128)(2,1)} %constant_dynamic-update-slice_fusion), calls=%async_computation | async-start | bytes 4194304 | tf_op jit(solution)/shard_map/all_to_all | solution.py:12
  111.9 1.3 fusion.40
  113.2 0.7 add_compare_fusion
  113.9 46.5 %all-to-all-done = bf16[128,8,1,1024]{3,1,2,0:T(8,128)(2,1)} async-done(((bf16[128,8,1,1024]{3,1,2,0:T(8,128)(2,1)}), bf16[128,8,1,1024]{3,1,2,0:T(8,128)(2,1)}, u32[]{:S(2)}, u32[]{:S(2)}) %all-to-all-start) | async-done | bytes 2097184 | tf_op jit(solution)/shard_map/all_to_all | solution.py:12
  160.3 2.0 %convert_reduce_fusion = f32[1024]{0:T(1024)S(1)} fusion(bf16[128,8,1,1024]{3,1,2,0:T(8,128)(2,1)} %all-to-all-done), kind=kLoop, calls=%fused_computation.3 | loop fusion | flops 2096128 | bytes 2101248 | tf_op jit(solution)/shard_map/reduce_sum | solution.py:35
  162.3 2.2 %fusion.6 = f32[1024]{0:T(1024)S(1)} fusion(bf16[128,8,1,1024]{3,1,2,0:T(8,128)(2,1)} %all-to-all-done, f32[1024]{0:T(1024)S(1)} %broadcast_multiply_fusion), kind=kLoop, calls=%fused_computation.11 | loop fusion | flops 4193280 | bytes 2105344 | tf_op jit(solution)/shard_map/reduce_sum | solution.py:37
  164.5 3.6 %fusion.21 = f32[64,1024]{1,0:T(8,128)S(1)} fusion(bf16[128,8,1,1024]{3,1,2,0:T(8,128)(2,1)} %all-to-all-done, f32[1024]{0:T(1024)S(1)} %add_rsqrt_fusion, f32[1024]{0:T(1024)S(1)} %broadcast_multiply_fusion, pred[1024]{0:T(1024)(128)(4,1)S(1)} %add_compare_fusion, f32[1,64,1024]{2,1,0:T(8,128)S(1)} %copy-done.2), kind=kOutput, calls=%fused_computation.26 | convolution fusion | flops 810549248 | bytes 2630656 | tf_op jit(solution)/shard_map/nbi,bri->brn/dot_general | solution.py:42
  168.1 5.7 %all-gather = f32[128,1024]{1,0:T(8,128)S(1)} all-gather(f32[64,1024]{1,0:T(8,128)S(1)} %fusion.21), channel_id=2, replica_groups=mesh['blk'=128,'row'=2] {'row'}, dimensions={0}, use_global_device_ids=true | all-gather | bytes 786432 | tf_op jit(solution)/shard_map/all_gather | solution.py:17
  173.8 3.0 %fusion.30 = f32[1,64,1024]{2,1,0:T(8,128)S(1)} fusion(f32[64,1024]{1,0:T(8,128)S(1)} %reduce.16, bf16[128,8,1,1024]{3,1,2,0:T(8,128)(2,1)} %all-to-all-done, f32[1024]{0:T(1024)S(1)} %add_rsqrt_fusion, f32[1024]{0:T(1024)S(1)} %broadcast_multiply_fusion, pred[1024]{0:T(1024)(128)(4,1)S(1)} %add_compare_fusion, f32[1,64,1024]{2,1,0:T(8,128)S(1)} %copy-done.2), kind=kOutput, calls=%fused_computation.29 | convolution fusion | flops 810811392 | bytes 2892800 | tf_op jit(solution)/shard_map/nbi,brn->bri/dot_general | solution.py:51
  177.2 1.9 all-gather.1
  179.3 5.8 %custom-call.8 = f32[1,64,64]{2,1,0:T(8,128)S(1)} custom-call(f32[1,64,64]{2,1,0:T(8,128)S(1)} %fusion.37), custom_call_target="Cholesky" | custom-call | tf_op jit(solution)/shard_map/jit(cholesky)/cholesky | solution.py:65
  185.2 0.6 compare_reduce_fusion
  185.8 1.3 fusion.39
  187.1 4.9 %custom-call.9 = f32[1,64,64]{1,2,0:T(8,128)S(1)} custom-call(f32[1,64,64]{2,1,0:T(8,128)S(1)} %get-tuple-element.3), custom_call_target="InvertDiagBlocksLowerTriangular" | custom-call | tf_op jit(solution)/shard_map/jit(_solve_triangular)/triangular_solve | solution.py:66
  192.0 1.1 convolution_bitcast_fusion
  (151 shorter events, 80.1 us)
Async XLA Ops:
  0.6 1.6 copy-start
  94.3 17.0 %copy-start.3 = (s32[128]{0:T(128)S(1)}, s32[128]{0:T(128)}, u32[]{:S(2)}) copy-start(s32[128]{0:T(128)} %param.5) | copy-start | bytes 1540
  94.3 17.6 %copy-start.4 = (s32[128]{0:T(128)S(1)}, s32[128]{0:T(128)}, u32[]{:S(2)}) copy-start(s32[128]{0:T(128)} %param.6) | copy-start | bytes 1540
  94.3 66.0 %all-to-all-start = ((bf16[128,8,1,1024]{3,1,2,0:T(8,128)(2,1)}), bf16[128,8,1,1024]{3,1,2,0:T(8,128)(2,1)}, u32[]{:S(2)}, u32[]{:S(2)}) async-start(bf16[128,8,1,1024]{3,1,2,0:T(8,128)(2,1)} %constant_dynamic-update-slice_fusion), calls=%async_computation | async-start | bytes 4194304 | tf_op jit(solution)/shard_map/all_to_all | solution.py:12
  113.9 50.7 %copy-start.2 = (f32[1,64,1024]{2,1,0:T(8,128)S(1)}, f32[1,64,1024]{2,1,0:T(8,128)}, u32[]{:S(2)}) copy-start(f32[1,64,1024]{2,1,0:T(8,128)} %param.7) | copy-start | bytes 786436
  176.8 16.3 %copy-start.1 = (f32[1,64,1024]{2,1,0:T(8,128)}, f32[1,64,1024]{2,1,0:T(8,128)S(1)}, u32[]{:S(2)}) copy-start(f32[1,64,1024]{2,1,0:T(8,128)S(1)} %fusion.30) | copy-start | bytes 786436
